TPU v7x, 32 devices: a whole 2x2x4 slice. The times are simulated.
32 devices in a mesh: row: 4 (over y, x), col: 8 (over z, core).
Axes of the slice: x: 2, y: 2, z: 4, core: 2. Of those that a mesh axis runs over, the one named last changes fastest.
Arguments:
- charge: float32 [256, 256, 256], P('col', 'row'), may hold values from -6 to 6
- green_spectrum: float32 [512, 512, 512], P('row', 'col'), may hold values from 0.2 to 2
Outputs:
- potential: float32 [256, 256, 256], P('col', 'row')
All inputs are finite; a program needn't handle non-finite values.
Results may differ from a plain program's by a relative error of at most 0.00007.
Values sent between devices are 32-bit elements; how exact they have to be, the bound alone decides.
A program may use at most 192 MiB of HBM per device.

v0:
```python
import math

import jax
import jax.numpy as jnp
from jax import lax
from jax.sharding import PartitionSpec as P

M = 512
N = 256


def phases(count_in, count_out, length):
    row_ids = lax.iota(jnp.int32, count_in)[:, None]
    col_ids = lax.iota(jnp.int32, count_out)[None, :]
    turn_ids = row_ids * col_ids % length
    angles = turn_ids.astype(jnp.float32) * (2.0 * math.pi / length)
    return (jnp.cos(angles), jnp.sin(angles))


def forward_table(count_in, count_out, length):
    cosine, sine_part = phases(count_in, count_out, length)
    return jnp.stack([jnp.stack([cosine, -sine_part], 1), jnp.stack([sine_part, cosine], 1)], 0)


def inverse_table(count_in, count_out, length):
    cosine, sine_part = phases(count_in, count_out, length)
    scaling = 1.0 / length
    return (
        jnp.stack([jnp.stack([cosine, sine_part], 1), jnp.stack([-sine_part, cosine], 1)], 0)
        * scaling
    )


def contract(pattern, left_side, right_side):
    return jnp.einsum(
        pattern,
        left_side,
        right_side,
        precision=lax.Precision.HIGHEST,
        preferred_element_type=jnp.float32,
    )


def on_device(charge, green_spectrum):
    cosine, sine_part = phases(N, M, M)
    real_table = jnp.stack([cosine, -sine_part], 1)
    along_z = contract("xyz,zqk->xyqk", charge, real_table)
    by_rows = lax.all_to_all(along_z, "row", split_axis=3, concat_axis=1, tiled=True)
    forward = forward_table(N, M, M)
    along_y = contract("xypk,pyqb->xkqb", by_rows, forward)
    spectrum = contract(
        "xkpj,pxqa->kjqa",
        lax.all_to_all(along_y, "col", split_axis=3, concat_axis=0, tiled=True),
        forward,
    )
    product = spectrum * green_spectrum[:, :, None, :]
    back_table = inverse_table(M, N, M)
    back_cos, back_sin = phases(M, N, M)
    real_back = jnp.stack([back_cos, -back_sin], 0) * (1.0 / M)
    back_x = contract("kjqa,qapx->kjpx", product, back_table)
    by_cols = lax.all_to_all(back_x, "col", split_axis=3, concat_axis=1, tiled=True)
    back_y = contract("kbpx,pbqy->kxqy", by_cols, back_table)
    return contract(
        "cxpy,pcz->xyz",
        lax.all_to_all(back_y, "row", split_axis=3, concat_axis=0, tiled=True),
        real_back,
    )


def solution(mesh):
    in_specs = (P("col", "row", None), P("row", "col", None))
    out_specs = P("col", "row", None)
    return jax.shard_map(
        on_device, mesh=mesh, in_specs=in_specs, out_specs=out_specs, check_vma=False
    )
```

profile of v0, /device:TPU:0, one launch (start us, length us, event | category | flops | bytes accessed | tf_op | source)
XLA Modules:
  0.0 1348.2 jit_solution(13706535293127981104)
XLA Ops:
  0.0 0.0 copy-start
  0.0 2.1 fusion.58
  2.1 0.0 copy-done
  2.1 9.0 convolution_bitcast_fusion.1
  11.1 16.2 %copy.38 = f32[32,64,2,512]{1,0,2,3:T(8,128)} copy(f32[32,64,2,512]{3,1,0,2:T(8,128)} %convolution_bitcast_fusion.1) | data formatting | bytes 16777216 | tf_op jit(solution)/shard_map/xyz,zqk->xyqk/dot_general | solution.py:35
  27.3 14.3 %reshape.237 = f32[4,1,524288]{2,1,0:T(1,128)} reshape(f32[512,2,32,64]{3,2,1,0:T(8,128)} %bitcast.107) | data formatting | bytes 16777216
  41.7 5.8 all-to-all-start
  47.5 1.9 fusion.57
  49.4 0.3 fusion.34
  49.7 91.6 %all-to-all-done = f32[4,1,524288]{2,1,0:T(1,128)} async-done(((f32[4,1,524288]{2,1,0:T(1,128)}), f32[4,1,524288]{2,1,0:T(1,128)}, u32[]{:S(2)}, u32[]{:S(2)}) %all-to-all-start) | async-done | bytes 8388640 | tf_op jit(solution)/shard_map/all_to_all | solution.py:48
  141.4 0.5 broadcast.343
  141.9 28.2 %reduce = f32[4,524288]{1,0:T(4,128)} reduce(f32[4,1,524288]{2,1,0:T(1,128)} %all-to-all-done, f32[]{:T(128)} %broadcast.343), dimensions={1}, to_apply=%all_to_all.52.reduce_sub_computation | reduce | bytes 16777220 | tf_op jit(solution)/shard_map/all_to_all | solution.py:48
  170.1 16.8 %reshape.238 = f32[512,2,32,64]{3,2,1,0:T(8,128)} reshape(f32[4,524288]{1,0:T(4,128)} %reduce) | data formatting | bytes 16777216
  186.9 12.8 copy.67
  199.6 4.7 copy.40
  204.3 30.4 %convolution_bitcast_fusion = f32[32,128,2,512]{3,1,2,0:T(8,128)} fusion(f32[32,256,2,128,1]{3,1,2,4,0:T(8,128)S(1)} %bitcast.111, f32[1,256,2,512]{3,1,2,0:T(8,128)S(1)} %get-tuple-element.8, f32[1,256,2,512]{3,1,2,0:T(8,128)S(1)} %get-tuple-element.7), kind=kOutput, calls=%fused_computation.9 | convolution fusion | flops 25770328064 | bytes 27262976 | tf_op jit(solution)/shard_map/xypk,pyqb->xkqb/dot_general | solution.py:35
  234.7 25.1 %copy.43 = f32[32,128,2,512]{1,2,0,3:T(2,128)} copy(f32[32,128,2,512]{3,1,2,0:T(8,128)} %convolution_bitcast_fusion) | data formatting | bytes 33554432 | tf_op jit(solution)/shard_map/xypk,pyqb->xkqb/dot_general | solution.py:35
  259.8 5.9 all-to-all-start.1
  265.7 17.7 %copy.48 = f32[128,64,512]{2,0,1:T(8,128)} copy(f32[128,64,512]{2,1,0:T(8,128)} %param.3) | data formatting | bytes 33554432 | tf_op args[1]
  283.4 1.9 fusion.60
  285.3 2.1 fusion.55
  287.4 1.5 fusion.78
  288.9 1.1 maximum_bitcast_fusion.1
  290.0 339.3 %all-to-all-done.1 = f32[32,128,2,512]{1,2,0,3:T(2,128)} async-done(((f32[32,128,2,512]{1,2,0,3:T(2,128)}), f32[32,128,2,512]{1,2,0,3:T(2,128)}, u32[]{:S(2)}, u32[]{:S(2)}) %all-to-all-start.1) | async-done | bytes 16777248 | tf_op jit(solution)/shard_map/all_to_all | solution.py:53
  629.3 11.0 copy.44
  640.3 0.0 copy-start.2
  640.3 1.8 copy.45
  642.1 0.0 copy-done.2
  642.1 0.0 copy-start.3
  642.1 71.3 %fusion.4 = f32[128,64,2,512,1]{3,0,4,2,1:T(8,128)} fusion(f32[256,128,2,64,1]{1,3,2,0,4:T(8,128)S(1)} %bitcast.106, f32[2,256,2,512,1]{3,1,0,2,4:T(8,128)S(1)} %copy-done.2), kind=kOutput, calls=%fused_computation.5 | convolution fusion | flops 51539607552 | bytes 52428800 | tf_op jit(solution)/shard_map/xkpj,pxqa->kjqa/dot_general | solution.py:35
  713.5 0.0 copy-done.3
  713.5 58.4 %fusion.7 = f32[128,64,2,256]{3,0,2,1:T(8,128)} fusion(f32[128,64,2,512,1]{3,0,4,2,1:T(8,128)} %fusion.4, f32[128,64,512]{2,0,1:T(8,128)} %copy.48, f32[1,512,2,256]{3,1,0,2:T(8,128)S(1)} %copy-done.3, f32[1,512,2,256]{3,1,0,2:T(8,128)S(1)} %get-tuple-element.5), kind=kOutput, calls=%fused_computation.8 | convolution fusion | flops 51549044736 | bytes 69206016 | tf_op jit(solution)/shard_map/kjqa,qapx->kjpx/dot_general | solution.py:35
  771.9 25.0 %copy.50 = f32[128,64,2,256]{0,2,1,3:T(2,128)} copy(f32[128,64,2,256]{3,0,2,1:T(8,128)} %fusion.7) | data formatting | bytes 33554432 | tf_op jit(solution)/shard_map/kjqa,qapx->kjpx/dot_general | solution.py:35
  796.9 367.8 %all_to_all.72 = f32[128,64,2,256]{0,2,1,3:T(2,128)S(1)} all-to-all(f32[128,64,2,256]{0,2,1,3:T(2,128)} %copy.50), channel_id=1, replica_groups=mesh['row'=4,'col'=8] {'col'}, dimensions={3} | all-to-all | bytes 33554432 | tf_op jit(solution)/shard_map/all_to_all | solution.py:61
  1164.7 10.3 copy.51
  1175.0 0.0 copy-start.4
  1175.0 7.0 copy.52
  1182.0 0.0 copy-done.4
  1182.0 37.7 %fusion.13 = f32[128,32,2,256]{3,0,2,1:T(8,128)} fusion(f32[128,512,2,32,1]{0,3,2,1,4:T(8,128)} %bitcast.114, f32[1,512,2,256]{3,1,0,2:T(8,128)S(1)} %copy-done.4, f32[1,512,2,256]{3,1,0,2:T(8,128)S(1)} %get-tuple-element.5), kind=kOutput, calls=%fused_computation.13 | convolution fusion | flops 25770852352 | bytes 27262976 | tf_op jit(solution)/shard_map/kbpx,pbqy->kxqy/dot_general | solution.py:35
  1219.6 13.2 copy.54
  1232.9 5.9 all-to-all-start.3
  1238.7 2.1 sine_negate_fusion
  1240.8 90.0 %all-to-all-done.3 = f32[128,32,2,256]{0,2,1,3:T(2,128)} async-done(((f32[128,32,2,256]{0,2,1,3:T(2,128)}), f32[128,32,2,256]{0,2,1,3:T(2,128)}, u32[]{:S(2)}, u32[]{:S(2)}) %all-to-all-start.3) | async-done | bytes 8388640 | tf_op jit(solution)/shard_map/all_to_all | solution.py:65
  1330.8 0.0 copy-start.1
  1330.8 8.4 copy.55
  1339.2 8.5 fusion.22
  1347.7 0.0 copy-done.1
Async XLA Ops:
  0.0 2.1 copy-start
  41.7 99.7 %all-to-all-start = ((f32[4,1,524288]{2,1,0:T(1,128)}), f32[4,1,524288]{2,1,0:T(1,128)}, u32[]{:S(2)}, u32[]{:S(2)}) async-start(f32[4,1,524288]{2,1,0:T(1,128)} %reshape.237), calls=%async_computation | async-start | bytes 16777216 | tf_op jit(solution)/shard_map/all_to_all | solution.py:48
  259.8 369.5 %all-to-all-start.1 = ((f32[32,128,2,512]{1,2,0,3:T(2,128)}), f32[32,128,2,512]{1,2,0,3:T(2,128)}, u32[]{:S(2)}, u32[]{:S(2)}) async-start(f32[32,128,2,512]{1,2,0,3:T(2,128)} %copy.43), calls=%async_computation.1 | async-start | bytes 33554432 | tf_op jit(solution)/shard_map/all_to_all | solution.py:53
  640.3 1.8 copy-start.2
  642.1 71.4 %copy-start.3 = (f32[1,512,2,256]{3,1,0,2:T(8,128)S(1)}, f32[1,512,2,256]{3,1,0,2:T(8,128)}, u32[]{:S(2)}) copy-start(f32[1,512,2,256]{3,1,0,2:T(8,128)} %get-tuple-element.6) | copy-start | bytes 3145732
  1175.0 7.0 copy-start.4
  1232.9 97.9 %all-to-all-start.3 = ((f32[128,32,2,256]{0,2,1,3:T(2,128)}), f32[128,32,2,256]{0,2,1,3:T(2,128)}, u32[]{:S(2)}, u32[]{:S(2)}) async-start(f32[128,32,2,256]{0,2,1,3:T(2,128)} %copy.54), calls=%async_computation.3 | async-start | bytes 16777216 | tf_op jit(solution)/shard_map/all_to_all | solution.py:65
  1330.8 16.9 %copy-start.1 = (f32[32,64,256]{2,1,0:T(8,128)S(1)}, f32[32,64,256]{2,1,0:T(8,128)}, u32[]{:S(2)}) copy-start(f32[32,64,256]{2,1,0:T(8,128)} %param.2) | copy-start | bytes 6291460
where the time goes:
time: 1360 us; the launch traced here: 1350 us
  waiting for transfers between devices  521 us (38%)
  blocking collectives  368 us (27%)
  matrix products  215 us (16%)
  local copies, waits for them, and re-layouts  185 us (14%)
  other arithmetic  41.2 us (3%)
  starting transfers between devices  17.6 us (1%)
    all_to_all x1, blocking collectives, on_device(): lax.all_to_all(back_x, 'col', split_axis=3, concat_axis=1, tiled=True)  368 us
    all_to_all x1, waiting for transfers between devices, on_device(): lax.all_to_all(along_y, 'col', split_axis=3, concat_axis=0, tiled=True)  339 us
    dot_general x6, matrix products, contract(): jnp.einsum(pattern, left_side, right_side, precision=lax.Precision.HIGHES...  215 us
    all_to_all x1, waiting for transfers between devices, on_device(): lax.all_to_all(along_z, 'row', split_axis=3, concat_axis=1, tiled=True)  91.6 us
    all_to_all x1, waiting for transfers between devices, on_device(): lax.all_to_all(back_y, 'row', split_axis=3, concat_axis=0, tiled=True)  90 us
    dot_general x4, local copies, waits for them, and re-layouts, contract(): jnp.einsum(pattern, left_side, right_side, precision=lax.Precision.HIGHES...  79.6 us
    unnamed x13, local copies, waits for them, and re-layouts  48.9 us
    all_to_all x1, other arithmetic, on_device(): lax.all_to_all(along_z, 'row', split_axis=3, concat_axis=1, tiled=True)  28.2 us
  transfers between devices with their start and end apart: 3, of which 3 were waited for; matrix products, arithmetic and copies ran while one was open for 2% of the time, Pallas kernels for 0%

commit v1 on v0

--- a/solution.py
+++ b/solution.py
@@ -36,7 +36,7 @@
         pattern,
         left_side,
         right_side,
-        precision=lax.Precision.HIGHEST,
+        precision=lax.Precision.HIGH,
         preferred_element_type=jnp.float32,
     )
 

time: 1360 us -> 1280 us (0.941)
  matrix products: 215 us -> 139 us
    dot_general x6, matrix products: 215 us -> 139 us  [contract(): jnp.einsum(pattern, left_side, right_side, precision=lax.Precision.HIGH,...]
    unnamed x13 -> x11, local copies, waits for them, and re-layouts: 48.9 us -> 48.9 us
where the time goes in v1:
time: 1280 us; the launch traced here: 1270 us
  waiting for transfers between devices  523 us (41%)
  blocking collectives  368 us (29%)
  local copies, waits for them, and re-layouts  185 us (14%)
  matrix products  139 us (11%)
  other arithmetic  39.7 us (3%)
  starting transfers between devices  17.2 us (1%)
    all_to_all x1, blocking collectives, on_device(): lax.all_to_all(back_x, 'col', split_axis=3, concat_axis=1, tiled=True)  368 us
    all_to_all x1, waiting for transfers between devices, on_device(): lax.all_to_all(along_y, 'col', split_axis=3, concat_axis=0, tiled=True)  341 us
    dot_general x6, matrix products, contract(): jnp.einsum(pattern, left_side, right_side, precision=lax.Precision.HIGH,...  139 us
    all_to_all x1, waiting for transfers between devices, on_device(): lax.all_to_all(along_z, 'row', split_axis=3, concat_axis=1, tiled=True)  91.6 us
    all_to_all x1, waiting for transfers between devices, on_device(): lax.all_to_all(back_y, 'row', split_axis=3, concat_axis=0, tiled=True)  90.2 us
    dot_general x4, local copies, waits for them, and re-layouts, contract(): jnp.einsum(pattern, left_side, right_side, precision=lax.Precision.HIGH,...  79.7 us
    unnamed x11, local copies, waits for them, and re-layouts  48.9 us
    all_to_all x1, other arithmetic, on_device(): lax.all_to_all(along_z, 'row', split_axis=3, concat_axis=1, tiled=True)  28.2 us
  transfers between devices with their start and end apart: 3, of which 3 were waited for; matrix products, arithmetic and copies ran while one was open for 2% of the time, Pallas kernels for 0%

profile of v1, /device:TPU:0, one launch (start us, length us, event | category | flops | bytes accessed | tf_op | source)
XLA Modules:
  0.0 1271.5 jit_solution(5702876776140178700)
XLA Ops:
  0.0 0.0 copy-start
  0.0 2.1 fusion.58
  2.1 0.0 copy-done
  2.1 5.7 convolution_bitcast_fusion.1
  7.8 16.3 %copy.38 = f32[32,64,2,512]{1,0,2,3:T(8,128)} copy(f32[32,64,2,512]{3,1,0,2:T(8,128)} %convolution_bitcast_fusion.1) | data formatting | bytes 16777216 | tf_op jit(solution)/shard_map/xyz,zqk->xyqk/dot_general | solution.py:35
  24.1 14.3 %reshape.237 = f32[4,1,524288]{2,1,0:T(1,128)} reshape(f32[512,2,32,64]{3,2,1,0:T(8,128)} %bitcast.92) | data formatting | bytes 16777216
  38.5 5.8 all-to-all-start
  44.3 1.9 fusion.57
  46.2 0.3 fusion.34
  46.5 91.6 %all-to-all-done = f32[4,1,524288]{2,1,0:T(1,128)} async-done(((f32[4,1,524288]{2,1,0:T(1,128)}), f32[4,1,524288]{2,1,0:T(1,128)}, u32[]{:S(2)}, u32[]{:S(2)}) %all-to-all-start) | async-done | bytes 8388640 | tf_op jit(solution)/shard_map/all_to_all | solution.py:48
  138.1 0.5 broadcast.343
  138.6 28.2 %reduce = f32[4,524288]{1,0:T(4,128)} reduce(f32[4,1,524288]{2,1,0:T(1,128)} %all-to-all-done, f32[]{:T(128)} %broadcast.343), dimensions={1}, to_apply=%all_to_all.52.reduce_sub_computation | reduce | bytes 16777220 | tf_op jit(solution)/shard_map/all_to_all | solution.py:48
  166.8 16.8 %reshape.238 = f32[512,2,32,64]{3,2,1,0:T(8,128)} reshape(f32[4,524288]{1,0:T(4,128)} %reduce) | data formatting | bytes 16777216
  183.6 12.8 %copy.67 = f32[32,64,2,4,128]{4,3,1,2,0:T(4,128)} copy(f32[32,64,2,4,128]{1,0,2,4,3:T(8,128)} %bitcast.93) | data formatting | bytes 16777216 | tf_op jit(solution)/shard_map/all_to_all | solution.py:48
  196.4 4.7 copy.40
  201.1 16.9 %convolution_bitcast_fusion = f32[32,128,2,512]{3,1,2,0:T(8,128)} fusion(f32[32,256,2,128,1]{3,1,2,4,0:T(8,128)S(1)} %bitcast.99, f32[1,256,2,512]{3,1,2,0:T(8,128)S(1)} %get-tuple-element.8, f32[1,256,2,512]{3,1,2,0:T(8,128)S(1)} %get-tuple-element.7), kind=kOutput, calls=%fused_computation.9 | convolution fusion | flops 12885426176 | bytes 27262976 | tf_op jit(solution)/shard_map/xypk,pyqb->xkqb/dot_general | solution.py:35
  218.0 25.1 %copy.43 = f32[32,128,2,512]{1,2,0,3:T(2,128)} copy(f32[32,128,2,512]{3,1,2,0:T(8,128)} %convolution_bitcast_fusion) | data formatting | bytes 33554432 | tf_op jit(solution)/shard_map/xypk,pyqb->xkqb/dot_general | solution.py:35
  243.0 5.7 all-to-all-start.1
  248.8 17.7 %copy.48 = f32[128,64,512]{2,0,1:T(8,128)} copy(f32[128,64,512]{2,1,0:T(8,128)} %param.3) | data formatting | bytes 33554432 | tf_op args[1]
  266.5 1.9 fusion.60
  268.4 2.1 fusion.55
  270.5 1.1 maximum_bitcast_fusion.1
  271.6 340.8 %all-to-all-done.1 = f32[32,128,2,512]{1,2,0,3:T(2,128)} async-done(((f32[32,128,2,512]{1,2,0,3:T(2,128)}), f32[32,128,2,512]{1,2,0,3:T(2,128)}, u32[]{:S(2)}, u32[]{:S(2)}) %all-to-all-start.1) | async-done | bytes 16777248 | tf_op jit(solution)/shard_map/all_to_all | solution.py:53
  612.4 11.0 copy.44
  623.4 1.8 copy.45
  625.2 0.0 copy-start.2
  625.2 45.0 %fusion.4 = f32[128,64,2,512,1]{3,0,4,2,1:T(8,128)} fusion(f32[256,128,2,64,1]{1,3,2,0,4:T(8,128)S(1)} %bitcast.91, f32[1,256,2,512]{3,1,2,0:T(8,128)S(1)} %get-tuple-element.8, f32[1,256,2,512]{3,1,2,0:T(8,128)S(1)} %get-tuple-element.7), kind=kOutput, calls=%fused_computation.5 | convolution fusion | flops 25770328064 | bytes 52428800 | tf_op jit(solution)/shard_map/xkpj,pxqa->kjqa/dot_general | solution.py:35
  670.2 0.0 copy-done.2
  670.3 33.9 %fusion.7 = f32[128,64,2,256]{3,0,2,1:T(8,128)} fusion(f32[128,64,2,512,1]{3,0,4,2,1:T(8,128)} %fusion.4, f32[128,64,512]{2,0,1:T(8,128)} %copy.48, f32[1,512,2,256]{3,1,0,2:T(8,128)S(1)} %copy-done.2, f32[1,512,2,256]{3,1,0,2:T(8,128)S(1)} %get-tuple-element.5), kind=kOutput, calls=%fused_computation.8 | convolution fusion | flops 25779240960 | bytes 69206016 | tf_op jit(solution)/shard_map/kjqa,qapx->kjpx/dot_general | solution.py:35
  704.2 25.1 %copy.50 = f32[128,64,2,256]{0,2,1,3:T(2,128)} copy(f32[128,64,2,256]{3,0,2,1:T(8,128)} %fusion.7) | data formatting | bytes 33554432 | tf_op jit(solution)/shard_map/kjqa,qapx->kjpx/dot_general | solution.py:35
  729.2 367.8 %all_to_all.72 = f32[128,64,2,256]{0,2,1,3:T(2,128)S(1)} all-to-all(f32[128,64,2,256]{0,2,1,3:T(2,128)} %copy.50), channel_id=1, replica_groups=mesh['row'=4,'col'=8] {'col'}, dimensions={3} | all-to-all | bytes 33554432 | tf_op jit(solution)/shard_map/all_to_all | solution.py:61
  1097.0 10.3 copy.51
  1107.3 0.0 copy-start.3
  1107.3 7.0 copy.52
  1114.3 0.0 copy-done.3
  1114.3 32.6 %fusion.13 = f32[128,32,2,256]{3,0,2,1:T(8,128)} fusion(f32[128,512,2,32,1]{0,3,2,1,4:T(8,128)} %bitcast.98, f32[1,512,2,256]{3,1,0,2:T(8,128)S(1)} %copy-done.3, f32[1,512,2,256]{3,1,0,2:T(8,128)S(1)} %get-tuple-element.5), kind=kOutput, calls=%fused_computation.13 | convolution fusion | flops 12885950464 | bytes 27262976 | tf_op jit(solution)/shard_map/kbpx,pbqy->kxqy/dot_general | solution.py:35
  1146.9 13.2 %copy.54 = f32[128,32,2,256]{0,2,1,3:T(2,128)} copy(f32[128,32,2,256]{3,0,2,1:T(8,128)} %fusion.13) | data formatting | bytes 16777216 | tf_op jit(solution)/shard_map/kbpx,pbqy->kxqy/dot_general | solution.py:35
  1160.1 5.7 all-to-all-start.3
  1165.8 2.1 sine_negate_fusion
  1167.9 90.2 %all-to-all-done.3 = f32[128,32,2,256]{0,2,1,3:T(2,128)} async-done(((f32[128,32,2,256]{0,2,1,3:T(2,128)}), f32[128,32,2,256]{0,2,1,3:T(2,128)}, u32[]{:S(2)}, u32[]{:S(2)}) %all-to-all-start.3) | async-done | bytes 8388640 | tf_op jit(solution)/shard_map/all_to_all | solution.py:65
  1258.1 0.0 copy-start.1
  1258.1 8.4 copy.55
  1266.5 4.9 fusion.22
  1271.3 0.0 copy-done.1
Async XLA Ops:
  0.0 2.1 copy-start
  38.5 99.7 %all-to-all-start = ((f32[4,1,524288]{2,1,0:T(1,128)}), f32[4,1,524288]{2,1,0:T(1,128)}, u32[]{:S(2)}, u32[]{:S(2)}) async-start(f32[4,1,524288]{2,1,0:T(1,128)} %reshape.237), calls=%async_computation | async-start | bytes 16777216 | tf_op jit(solution)/shard_map/all_to_all | solution.py:48
  243.0 369.4 %all-to-all-start.1 = ((f32[32,128,2,512]{1,2,0,3:T(2,128)}), f32[32,128,2,512]{1,2,0,3:T(2,128)}, u32[]{:S(2)}, u32[]{:S(2)}) async-start(f32[32,128,2,512]{1,2,0,3:T(2,128)} %copy.43), calls=%async_computation.1 | async-start | bytes 33554432 | tf_op jit(solution)/shard_map/all_to_all | solution.py:53
  625.2 45.1 %copy-start.2 = (f32[1,512,2,256]{3,1,0,2:T(8,128)S(1)}, f32[1,512,2,256]{3,1,0,2:T(8,128)}, u32[]{:S(2)}) copy-start(f32[1,512,2,256]{3,1,0,2:T(8,128)} %get-tuple-element.6) | copy-start | bytes 3145732
  1107.3 7.0 copy-start.3
  1160.1 97.9 %all-to-all-start.3 = ((f32[128,32,2,256]{0,2,1,3:T(2,128)}), f32[128,32,2,256]{0,2,1,3:T(2,128)}, u32[]{:S(2)}, u32[]{:S(2)}) async-start(f32[128,32,2,256]{0,2,1,3:T(2,128)} %copy.54), calls=%async_computation.3 | async-start | bytes 16777216 | tf_op jit(solution)/shard_map/all_to_all | solution.py:65
  1258.1 13.3 %copy-start.1 = (f32[32,64,256]{2,1,0:T(8,128)S(1)}, f32[32,64,256]{2,1,0:T(8,128)}, u32[]{:S(2)}) copy-start(f32[32,64,256]{2,1,0:T(8,128)} %param.2) | copy-start | bytes 6291460
